TPU v7x, 32 devices: a whole 2x2x4 slice. The times are simulated.
32 devices in a mesh: rows: 4 (over y, core), vecs: 8 (over z, x).
Axes of the slice: x: 2, y: 2, z: 4, core: 2. Of those that a mesh axis runs over, the one named last changes fastest.
Arguments:
- vectors: float32 [2048, 2048], P('rows', 'vecs'), may hold values from -6 to 6
- reflectors: float32 [4, 8, 512, 256], P(None, 'rows', 'vecs'), may hold values from -0.4 to 1, as said below
Outputs:
- transformed: float32 [2048, 2048], P('rows', 'vecs')
Inputs may be any that keep to these rules, and one draw needn't show every extreme that they name: reflectors[t, b] is unit lower trapezoidal: entry (i, j) is 1 where i == j and 0 where i < j.
All inputs are finite; a program needn't handle non-finite values.
Results may differ from a plain program's by a relative error of at most 0.00026.
Values sent between devices are 32-bit elements; how exact they have to be, the bound alone decides.
No kernel may reach another device: no remote copies, remote signals or barrier semaphores. Data moves between devices by JAX's collectives and lax.ppermute only.
A program may use at most 128 MiB of HBM per device.

v0:
```python
import jax
import jax.numpy as jnp
from jax import lax
from jax.sharding import PartitionSpec as P


def passed_along(value, axis, steps):
    count = lax.axis_size(axis)
    leading, last = (max(0, -steps), min(count, count - steps))
    return lax.ppermute(value, axis, [(source, source + steps) for source in range(leading, last)])


def invert_upper(matrix):
    size = matrix.shape[-1]
    if size == 1:
        return 1.0 / matrix
    half = size // 2
    upper_left = matrix[:, :half, :half]
    corner = matrix[:, :half, half:]
    lower_right = matrix[:, half:, half:]
    if half * 2 == size:
        count = matrix.shape[0]
        both = invert_upper(jnp.concatenate([upper_left, lower_right], axis=0))
        left_inverse = both[:count]
        right_inverse = both[count:]
    else:
        left_inverse = invert_upper(upper_left)
        right_inverse = invert_upper(lower_right)
    middle = jnp.einsum("bij,bjk->bik", corner, right_inverse, precision=lax.Precision.HIGHEST)
    middle = -jnp.einsum("bij,bjk->bik", left_inverse, middle, precision=lax.Precision.HIGHEST)
    zeros_block = jnp.zeros((matrix.shape[0], size - half, half), matrix.dtype)
    top = jnp.concatenate([left_inverse, middle], axis=2)
    bottom = jnp.concatenate([zeros_block, right_inverse], axis=2)
    return jnp.concatenate([top, bottom], axis=1)


def make_inverses(gram_full):
    diagonal = jnp.diagonal(gram_full, axis1=1, axis2=2)
    identity = jnp.eye(gram_full.shape[-1], dtype=gram_full.dtype)
    factors = jnp.triu(gram_full, 1) + 0.5 * identity * diagonal[:, None, :]
    return invert_upper(factors)


def reflect(window_rows, vblock, inverse):
    products = jnp.einsum("ri,rc->ic", vblock, window_rows, precision=lax.Precision.HIGHEST)
    solved = jnp.dot(inverse, products, precision=lax.Precision.HIGHEST)
    return window_rows - jnp.dot(vblock, solved, precision=lax.Precision.HIGHEST)


def local(vectors, reflectors):
    rows_dev = vectors.shape[0]
    block_count = reflectors.shape[1]
    width = reflectors.shape[3]
    topmost = lax.axis_index("rows") == 0
    lowest = lax.axis_index("rows") == lax.axis_size("rows") - 1
    tail_rows = jnp.zeros((width, vectors.shape[1]), jnp.float32)
    current = vectors
    for moment in range(reflectors.shape[0]):
        blocks = lax.all_gather(reflectors[moment], "vecs", axis=1, tiled=True)
        gram_full = jnp.einsum("bri,brj->bij", blocks, blocks, precision=lax.Precision.HIGHEST)
        inverses = make_inverses(gram_full)
        current = current.at[: 2 * width].set(reflect(current[: 2 * width], blocks[0], inverses[0]))
        shifted = passed_along(current[:width], "rows", -1)
        beneath = jnp.where(lowest, tail_rows, shifted)
        for column in range(1, block_count - 1):
            start = column * width
            current = current.at[start : start + 2 * width].set(
                reflect(current[start : start + 2 * width], blocks[column], inverses[column])
            )
        joined = jnp.concatenate([current[rows_dev - width :], beneath], axis=0)
        joined = reflect(joined, blocks[block_count - 1], inverses[block_count - 1])
        tail_rows = joined[width:]
        returned = passed_along(joined[width:], "rows", 1)
        current = jnp.concatenate(
            [
                jnp.where(topmost, current[:width], returned),
                current[width : rows_dev - width],
                joined[:width],
            ],
            axis=0,
        )
    return current


def solution(mesh):
    placed = (P("rows", "vecs"), P(None, "rows", "vecs", None))
    return jax.shard_map(
        local, mesh=mesh, in_specs=placed, out_specs=P("rows", "vecs"), check_vma=False
    )
```

profile of v0, /device:TPU:1, one launch (start us, length us, event | category | flops | bytes accessed | tf_op | source)
XLA Modules:
  0.0 346.5 jit_solution(13398819570180120822)
XLA Ops:
  12.8 37.4 %all-gather.9.cloned.1.call-done = f32[1,2,512,256]{3,2,1,0:T(8,128)} async-done(((f32[1,2,64,256]{3,2,1,0:T(8,128)}), f32[1,2,512,256]{3,2,1,0:T(8,128)}) %all-gather.9.cloned.1.call-update) | async-done | bytes 1048592 | tf_op jit(solution)/shard_map/all_gather | solution.py:59
  50.2 3.4 fusion.14
  53.6 16.6 %copy.201 = f32[2,256,256]{0,2,1:T(8,128)} copy(f32[2,256,256]{2,1,0:T(8,128)S(1)} %fusion.14) | data formatting | bytes 1048576 | tf_op jit(solution)/shard_map/bri,brj->bij/dot_general | solution.py:60
  70.1 2.3 gather_fusion
  72.5 18.8 %all-gather.11.cloned.1.call-done = f32[1,2,512,256]{3,2,1,0:T(8,128)} async-done(((f32[1,2,64,256]{3,2,1,0:T(8,128)}), f32[1,2,512,256]{3,2,1,0:T(8,128)}) %all-gather.11.cloned.1.call-update) | async-done | bytes 1048592 | tf_op jit(solution)/shard_map/all_gather | solution.py:59
  91.4 3.4 fusion.12
  94.8 16.3 %copy.213 = f32[2,256,256]{0,2,1:T(8,128)} copy(f32[2,256,256]{2,1,0:T(8,128)S(1)} %fusion.12) | data formatting | bytes 1048576 | tf_op jit(solution)/shard_map/bri,brj->bij/dot_general | solution.py:60
  111.1 2.3 gather_fusion.1
  113.5 19.0 %all-gather.13.cloned.1.call-done = f32[1,2,512,256]{3,2,1,0:T(8,128)} async-done(((f32[1,2,64,256]{3,2,1,0:T(8,128)}), f32[1,2,512,256]{3,2,1,0:T(8,128)}) %all-gather.13.cloned.1.call-update) | async-done | bytes 1048592 | tf_op jit(solution)/shard_map/all_gather | solution.py:59
  132.6 3.5 %fusion.10 = f32[2,256,256]{2,1,0:T(8,128)S(1)} fusion(f32[1,2,512,256]{3,2,1,0:T(8,128)} %all-gather.13.cloned.1.call-done), kind=kOutput, calls=%fused_computation.50 | convolution fusion | flops 805306368 | bytes 1572864 | tf_op jit(solution)/shard_map/bri,brj->bij/dot_general | solution.py:60
  136.0 16.3 %copy.224 = f32[2,256,256]{0,2,1:T(8,128)} copy(f32[2,256,256]{2,1,0:T(8,128)S(1)} %fusion.10) | data formatting | bytes 1048576 | tf_op jit(solution)/shard_map/bri,brj->bij/dot_general | solution.py:60
  154.8 18.8 %all-gather.15.cloned.1.call-done = f32[1,2,512,256]{3,2,1,0:T(8,128)} async-done(((f32[1,2,64,256]{3,2,1,0:T(8,128)}), f32[1,2,512,256]{3,2,1,0:T(8,128)}) %all-gather.15.cloned.1.call-update) | async-done | bytes 1048592 | tf_op jit(solution)/shard_map/all_gather | solution.py:59
  173.6 3.4 fusion.8
  177.0 16.7 %copy.235 = f32[2,256,256]{0,2,1:T(8,128)} copy(f32[2,256,256]{2,1,0:T(8,128)S(1)} %fusion.8) | data formatting | bytes 1048576 | tf_op jit(solution)/shard_map/bri,brj->bij/dot_general | solution.py:60
  193.8 2.3 gather_fusion.3
  267.6 4.3 %collective-permute-start = (f32[256,256]{0,1:T(8,128)S(1)}, f32[256,256]{0,1:T(8,128)S(1)}, u32[]{:S(2)}, u32[]{:S(2)}) collective-permute-start(f32[256,256]{0,1:T(8,128)S(1)} %get-tuple-element.106), channel_id=1, source_target_pairs={{8,0},{16,8},{24,16},{9,1},{17,9},{25,17},{10,2},{18,10},{26,18},{... | collective-permute-start | bytes 786440 | tf_op jit(solution)/shard_map/ppermute | solution.py:10
  274.1 2.9 collective-permute-done
  281.5 2.9 collective-permute-done.1
  290.5 4.6 %collective-permute-done.2 = f32[256,256]{0,1:T(8,128)S(1)} collective-permute-done((f32[256,256]{0,1:T(8,128)S(1)}, f32[256,256]{0,1:T(8,128)S(1)}, u32[]{:S(2)}, u32[]{:S(2)}) %collective-permute-start.2) | collective-permute-done | bytes 262176 | tf_op jit(solution)/shard_map/ppermute | solution.py:10
  299.3 3.1 collective-permute-done.3
  308.2 4.8 %collective-permute-done.4 = f32[256,256]{0,1:T(8,128)S(1)} collective-permute-done((f32[256,256]{0,1:T(8,128)S(1)}, f32[256,256]{0,1:T(8,128)S(1)}, u32[]{:S(2)}, u32[]{:S(2)}) %collective-permute-start.4) | collective-permute-done | bytes 262176 | tf_op jit(solution)/shard_map/ppermute | solution.py:10
  317.2 3.2 collective-permute-done.5
  324.6 6.5 %collective-permute-done.6 = f32[256,256]{0,1:T(8,128)S(1)} collective-permute-done((f32[256,256]{0,1:T(8,128)S(1)}, f32[256,256]{0,1:T(8,128)S(1)}, u32[]{:S(2)}, u32[]{:S(2)}) %collective-permute-start.6) | collective-permute-done | bytes 262176 | tf_op jit(solution)/shard_map/ppermute | solution.py:10
  335.2 3.3 collective-permute-done.7
  (291 shorter events, 115.2 us)
Async XLA Ops:
  6.5 43.6 %all-gather.9.cloned.1.call-start = ((), (), s32[]{:S(2)}) async-start(), calls=%async_computation | async-start | bytes 1179648 | tf_op jit(solution)/shard_map/all_gather | solution.py:59
  8.5 82.9 %all-gather.11.cloned.1.call-start = ((), (), s32[]{:S(2)}) async-start(), calls=%async_computation.1 | async-start | bytes 1179648 | tf_op jit(solution)/shard_map/all_gather | solution.py:59
  9.2 123.3 %all-gather.13.cloned.1.call-start = ((), (), s32[]{:S(2)}) async-start(), calls=%async_computation.2 | async-start | bytes 1179648 | tf_op jit(solution)/shard_map/all_gather | solution.py:59
  10.0 163.6 %all-gather.15.cloned.1.call-start = ((), (), s32[]{:S(2)}) async-start(), calls=%async_computation.3 | async-start | bytes 1179648 | tf_op jit(solution)/shard_map/all_gather | solution.py:59
  197.4 20.0 %copy-start.9 = (f32[2,256,256]{2,1,0:T(8,128)S(1)}, f32[2,256,256]{2,1,0:T(8,128)}, u32[]{:S(2)}) copy-start(f32[2,256,256]{2,1,0:T(8,128)} %get-tuple-element.116) | copy-start | bytes 1572868
  197.4 20.0 %copy-start.10 = (f32[2,256,256]{2,1,0:T(8,128)S(1)}, f32[2,256,256]{2,1,0:T(8,128)}, u32[]{:S(2)}) copy-start(f32[2,256,256]{2,1,0:T(8,128)} %get-tuple-element.114) | copy-start | bytes 1572868
  213.1 49.9 %copy-start.3 = (f32[1,2,512,256]{3,2,1,0:T(8,128)S(1)}, f32[1,2,512,256]{3,2,1,0:T(8,128)}, u32[]{:S(2)}) copy-start(f32[1,2,512,256]{3,2,1,0:T(8,128)} %all-gather.9.cloned.1.call-done) | copy-start | bytes 3145732
  220.5 64.0 %copy-start.2 = (f32[1,2,512,256]{3,2,1,0:T(8,128)S(1)}, f32[1,2,512,256]{3,2,1,0:T(8,128)}, u32[]{:S(2)}) copy-start(f32[1,2,512,256]{3,2,1,0:T(8,128)} %all-gather.11.cloned.1.call-done) | copy-start | bytes 3145732
  224.9 77.5 %copy-start.1 = (f32[1,2,512,256]{3,2,1,0:T(8,128)S(1)}, f32[1,2,512,256]{3,2,1,0:T(8,128)}, u32[]{:S(2)}) copy-start(f32[1,2,512,256]{3,2,1,0:T(8,128)} %all-gather.13.cloned.1.call-done) | copy-start | bytes 3145732
  245.4 35.7 %copy-start.21 = (f32[4,64,64]{2,1,0:T(8,128)S(1)}, f32[4,64,64]{2,1,0:T(8,128)}, u32[]{:S(2)}) copy-start(f32[4,64,64]{2,1,0:T(8,128)} %get-tuple-element.139) | copy-start | bytes 196612
  245.4 35.7 %copy-start.22 = (f32[4,64,64]{2,1,0:T(8,128)S(1)}, f32[4,64,64]{2,1,0:T(8,128)}, u32[]{:S(2)}) copy-start(f32[4,64,64]{2,1,0:T(8,128)} %get-tuple-element.140) | copy-start | bytes 196612
  245.4 35.8 %copy-start.5 = (f32[8,64,64]{2,1,0:T(8,128)S(1)}, f32[8,64,64]{2,1,0:T(8,128)}, u32[]{:S(2)}) copy-start(f32[8,64,64]{2,1,0:T(8,128)} %copy-done.4) | copy-start | bytes 393220
  245.4 35.8 %copy-start.23 = (f32[4,64,64]{2,1,0:T(8,128)S(1)}, f32[4,64,64]{2,1,0:T(8,128)}, u32[]{:S(2)}) copy-start(f32[4,64,64]{2,1,0:T(8,128)} %fusion.67) | copy-start | bytes 196612
  245.4 53.7 %copy-start.19 = (f32[4,64,64]{2,1,0:T(8,128)S(1)}, f32[4,64,64]{2,1,0:T(8,128)}, u32[]{:S(2)}) copy-start(f32[4,64,64]{2,1,0:T(8,128)} %get-tuple-element.119) | copy-start | bytes 196612
  245.4 53.7 %copy-start.20 = (f32[4,64,64]{2,1,0:T(8,128)S(1)}, f32[4,64,64]{2,1,0:T(8,128)}, u32[]{:S(2)}) copy-start(f32[4,64,64]{2,1,0:T(8,128)} %get-tuple-element.120) | copy-start | bytes 196612
  249.3 71.1 %copy-start = (f32[1,2,512,256]{3,2,1,0:T(8,128)S(1)}, f32[1,2,512,256]{3,2,1,0:T(8,128)}, u32[]{:S(2)}) copy-start(f32[1,2,512,256]{3,2,1,0:T(8,128)} %all-gather.15.cloned.1.call-done) | copy-start | bytes 3145732
  267.6 9.4 %collective-permute-start = (f32[256,256]{0,1:T(8,128)S(1)}, f32[256,256]{0,1:T(8,128)S(1)}, u32[]{:S(2)}, u32[]{:S(2)}) collective-permute-start(f32[256,256]{0,1:T(8,128)S(1)} %get-tuple-element.106), channel_id=1, source_target_pairs={{8,0},{16,8},{24,16},{9,1},{17,9},{25,17},{10,2},{18,10},{26,18},{... | collective-permute-start | bytes 786440 | tf_op jit(solution)/shard_map/ppermute | solution.py:10
  279.2 5.2 %collective-permute-start.1 = (f32[256,256]{0,1:T(8,128)S(1)}, f32[256,256]{0,1:T(8,128)S(1)}, u32[]{:S(2)}, u32[]{:S(2)}) collective-permute-start(f32[256,256]{0,1:T(8,128)S(1)} %get-tuple-element.103), channel_id=1, source_target_pairs={{0,8},{8,16},{16,24},{1,9},{9,17},{17,25},{2,10},{10,18},{18,26},{... | collective-permute-start | bytes 786440 | tf_op jit(solution)/shard_map/ppermute | solution.py:10
  286.6 8.4 %collective-permute-start.2 = (f32[256,256]{0,1:T(8,128)S(1)}, f32[256,256]{0,1:T(8,128)S(1)}, u32[]{:S(2)}, u32[]{:S(2)}) collective-permute-start(f32[256,256]{0,1:T(8,128)S(1)} %get-tuple-element.100), channel_id=1, source_target_pairs={{8,0},{16,8},{24,16},{9,1},{17,9},{25,17},{10,2},{18,10},{26,18},{... | collective-permute-start | bytes 786440 | tf_op jit(solution)/shard_map/ppermute | solution.py:10
  297.2 5.2 %collective-permute-start.3 = (f32[256,256]{0,1:T(8,128)S(1)}, f32[256,256]{0,1:T(8,128)S(1)}, u32[]{:S(2)}, u32[]{:S(2)}) collective-permute-start(f32[256,256]{0,1:T(8,128)S(1)} %get-tuple-element.97), channel_id=1, source_target_pairs={{0,8},{8,16},{16,24},{1,9},{9,17},{17,25},{2,10},{10,18},{18,26},{... | collective-permute-start | bytes 786440 | tf_op jit(solution)/shard_map/ppermute | solution.py:10
  304.6 8.4 %collective-permute-start.4 = (f32[256,256]{0,1:T(8,128)S(1)}, f32[256,256]{0,1:T(8,128)S(1)}, u32[]{:S(2)}, u32[]{:S(2)}) collective-permute-start(f32[256,256]{0,1:T(8,128)S(1)} %get-tuple-element.94), channel_id=1, source_target_pairs={{8,0},{16,8},{24,16},{9,1},{17,9},{25,17},{10,2},{18,10},{26,18},{... | collective-permute-start | bytes 786440 | tf_op jit(solution)/shard_map/ppermute | solution.py:10
  315.2 5.2 %collective-permute-start.5 = (f32[256,256]{0,1:T(8,128)S(1)}, f32[256,256]{0,1:T(8,128)S(1)}, u32[]{:S(2)}, u32[]{:S(2)}) collective-permute-start(f32[256,256]{0,1:T(8,128)S(1)} %get-tuple-element.91), channel_id=1, source_target_pairs={{0,8},{8,16},{16,24},{1,9},{9,17},{17,25},{2,10},{10,18},{18,26},{... | collective-permute-start | bytes 786440 | tf_op jit(solution)/shard_map/ppermute | solution.py:10
  322.6 8.4 %collective-permute-start.6 = (f32[256,256]{0,1:T(8,128)S(1)}, f32[256,256]{0,1:T(8,128)S(1)}, u32[]{:S(2)}, u32[]{:S(2)}) collective-permute-start(f32[256,256]{0,1:T(8,128)S(1)} %get-tuple-element.88), channel_id=1, source_target_pairs={{8,0},{16,8},{24,16},{9,1},{17,9},{25,17},{10,2},{18,10},{26,18},{... | collective-permute-start | bytes 786440 | tf_op jit(solution)/shard_map/ppermute | solution.py:10
  333.2 5.2 %collective-permute-start.7 = (f32[256,256]{0,1:T(8,128)S(1)}, f32[256,256]{0,1:T(8,128)S(1)}, u32[]{:S(2)}, u32[]{:S(2)}) collective-permute-start(f32[256,256]{0,1:T(8,128)S(1)} %get-tuple-element.85), channel_id=1, source_target_pairs={{0,8},{8,16},{16,24},{1,9},{9,17},{17,25},{2,10},{10,18},{18,26},{... | collective-permute-start | bytes 786440 | tf_op jit(solution)/shard_map/ppermute | solution.py:10
  (12 other events, 12.7 us)
Sparse Core Ops, SparseCore 0:
  9.5 40.6 all-gather.8
  52.3 38.9 all-gather.10
  93.5 38.9 all-gather.12
  134.6 38.9 all-gather.14
where the time goes:
time: 350 us; the launch traced here: 347 us
  waiting for transfers between devices  127 us (36%)
  local copies, waits for them, and re-layouts  96.6 us (28%)
  matrix products  74 us (21%)
  starting transfers between devices  18.1 us (5%)
  other arithmetic  15.6 us (4%)
  between operations  15.1 us (4%)
    all_gather x4, waiting for transfers between devices, local(): blocks = lax.all_gather(reflectors[moment], 'vecs', axis=1, tiled=True)  94.1 us
    dot_general x4, local copies, waits for them, and re-layouts, local(): jnp.einsum('bri,brj->bij', blocks, blocks, precision=lax.Precision.HIGHEST)  66 us
    ppermute x8, waiting for transfers between devices, passed_along(): lax.ppermute(value, axis, [(source, source + steps) for source in range(l...  31.2 us
    dot_general x28, matrix products, invert_upper(): jnp.einsum('bij,bjk->bik', corner, right_inverse, precision=lax.Precision...  26.2 us
    ppermute x8, starting transfers between devices, passed_along(): lax.ppermute(value, axis, [(source, source + steps) for source in range(l...  18 us
    dot_general x28, matrix products, invert_upper(): jnp.einsum('bij,bjk->bik', left_inverse, middle, precision=lax.Precision....  15 us
    dot_general x4, matrix products, local(): jnp.einsum('bri,brj->bij', blocks, blocks, precision=lax.Precision.HIGHEST)  13.7 us
    gather x8, local copies, waits for them, and re-layouts, make_inverses(): diagonal = jnp.diagonal(gram_full, axis1=1, axis2=2)  9.59 us
  transfers between devices with their start and end apart: 12, of which 12 were waited for; matrix products, arithmetic and copies ran while one was open for 22% of the time, Pallas kernels for 0%

commit v1 on v0

v1 whole, which is shorter than its diff:
```python
import functools

import jax
import jax.numpy as jnp
from jax import lax
from jax.experimental import pallas as pl
from jax.experimental.pallas import tpu as pltpu
from jax.sharding import PartitionSpec as P

BASE = 16
BF = jnp.bfloat16
F32 = jnp.float32


def split(value):
    high = value.astype(BF)
    return high, (value - high.astype(F32)).astype(BF)


def dot3(left, right, dims=((1,), (0,))):
    (lh, ll), (rh, rl) = left, right
    run = functools.partial(lax.dot_general, dimension_numbers=(dims, ((), ())), preferred_element_type=F32)
    return run(lh, rh) + (run(lh, rl) + run(ll, rh))


def invert_factor(gram):
    size = gram.shape[0]
    count = size // BASE
    row = lax.broadcasted_iota(jnp.int32, (size, size), 0)
    col = lax.broadcasted_iota(jnp.int32, (size, size), 1)
    factor = jnp.where(row < col, gram, jnp.where(row == col, 0.5 * gram, 0.0))
    same = (row // BASE) == (col // BASE)
    blocks = jnp.where(same, factor, 0.0)
    compact = jnp.sum(blocks.reshape(count, BASE, size), axis=0)
    lane = lax.broadcasted_iota(jnp.int32, (BASE, size), 1) % BASE
    sub = lax.broadcasted_iota(jnp.int32, (BASE, size), 0)
    ones = same.astype(BF)
    stacked = jnp.concatenate([jnp.where(lane == k, compact, 0.0) for k in range(BASE)], axis=0)
    high, low = split(stacked)
    rest = (stacked - high.astype(F32) - low.astype(F32)).astype(BF)
    run = functools.partial(jnp.dot, preferred_element_type=F32)
    spread = run(high, ones) + (run(low, ones) + run(rest, ones))
    small = jnp.where(sub == lane, 1.0, 0.0).astype(F32)
    for k in reversed(range(BASE)):
        column = spread[BASE * k : BASE * (k + 1)]
        pivot = small[k : k + 1] / column[k : k + 1]
        small = jnp.where(sub == k, pivot, small - jnp.where(sub < k, column, 0.0) * pivot)
    inverse = jnp.where(same, jnp.concatenate([small] * count, axis=0), 0.0)
    width = BASE
    while width < size:
        corner = jnp.where(((row // width) % 2 == 0) & ((col // width) == (row // width) + 1), factor, 0.0)
        parts = split(inverse)
        middle = dot3(split(corner), parts)
        inverse = inverse - dot3(parts, split(middle))
        width *= 2
    return inverse


def prepare_kernel(place_ref, *refs, groups):
    chunks = refs[: groups + 1]
    vh_ref, vl_ref, wh_ref, wl_ref, shared_ref, full_ref = refs[groups + 1 :]
    rows = chunks[0].shape[1]
    place = place_ref[0]
    block_count = full_ref.shape[0]
    for k in range(groups):
        line = lax.rem(place // 2 - k + groups, groups) * 2
        own = pl.multiple_of((line + place % 2) * rows, rows)
        other = pl.multiple_of((line + 1 - place % 2) * rows, rows)
        full_ref[:, pl.ds(own, rows), :] = chunks[k][...]
        full_ref[:, pl.ds(other, rows), :] = chunks[groups][k]
    width = full_ref.shape[2]
    parts = []
    for b in range(block_count):
        high, low = split(full_ref[b])
        vh_ref[b] = high
        vl_ref[b] = low
        parts.append((high, low))
    grams = [dot3(v, v, ((0,), (0,))) for v in parts]
    inverses = [invert_factor(g) for g in grams]
    for b in range(block_count):
        weights = dot3(split(inverses[b]), parts[b], ((1,), (1,)))
        wparts = split(weights)
        wh_ref[b] = wparts[0]
        wl_ref[b] = wparts[1]
        if b == block_count - 1:
            bottom = (parts[b][0][width:], parts[b][1][width:])
            shared_ref[...] = dot3(bottom, wparts)


def prepare(place, zs, xs):
    groups = len(zs)
    block_count, rows, width = zs[0].shape
    total = rows * groups * 2
    vm = pl.BlockSpec(memory_space=pltpu.VMEM)
    flops = block_count * 3 * 2 * (total * width * width * 2 + 10 * width**3)
    return pl.pallas_call(
        functools.partial(prepare_kernel, groups=groups),
        in_specs=[pl.BlockSpec(memory_space=pltpu.SMEM)] + [vm] * (groups + 1),
        out_specs=[vm] * 5,
        out_shape=[
            jax.ShapeDtypeStruct((block_count, total, width), BF),
            jax.ShapeDtypeStruct((block_count, total, width), BF),
            jax.ShapeDtypeStruct((block_count, width, total), BF),
            jax.ShapeDtypeStruct((block_count, width, total), BF),
            jax.ShapeDtypeStruct((width, total), F32),
        ],
        scratch_shapes=[pltpu.VMEM((block_count, total, width), F32)],
        cost_estimate=pl.CostEstimate(flops=flops, bytes_accessed=8 * block_count * total * width, transcendentals=0),
        name="prepare",
    )(place, *zs, xs)


def first_kernel(vh, vl, wh, wl, upper, lower, out_upper, out_lower):
    width = upper.shape[0]
    rows = jnp.concatenate([upper[...], lower[...]], axis=0)
    solved = dot3((wh[0], wl[0]), split(rows))
    change = dot3((vh[0], vl[0]), split(solved))
    out_upper[...] = upper[...] - change[:width]
    out_lower[...] = lower[...] - change[width:]


def first(made, upper, lower):
    vm = pl.BlockSpec(memory_space=pltpu.VMEM)
    vh, vl, wh, wl, _ = made
    out = jax.ShapeDtypeStruct(upper.shape, F32)
    return pl.pallas_call(
        first_kernel,
        in_specs=[vm] * 6,
        out_specs=[vm] * 2,
        out_shape=[out, out],
        cost_estimate=pl.CostEstimate(flops=6 * vh.shape[1] * vh.shape[2] * upper.shape[1] * 2, bytes_accessed=0, transcendentals=0),
        name="first",
    )(vh, vl, wh, wl, upper, lower)


def second_kernel(vh, vl, wh, wl, shared, sent, lower, above, beneath, out_shared, out_lower):
    last = vh.shape[0] - 1
    width = lower.shape[0]
    rows = jnp.concatenate([lower[...], beneath[...]], axis=0)
    solved = dot3((wh[last], wl[last]), split(rows))
    change = dot3((vh[last, :width], vl[last, :width]), split(solved))
    out_lower[...] = lower[...] - change
    both = jnp.concatenate([above[...], sent[...]], axis=0)
    out_shared[...] = sent[...] - dot3(split(shared[...]), split(both))


def second(made, shared, sent, lower, above, beneath):
    vm = pl.BlockSpec(memory_space=pltpu.VMEM)
    vh, vl, wh, wl, _ = made
    out = jax.ShapeDtypeStruct(lower.shape, F32)
    return pl.pallas_call(
        second_kernel,
        in_specs=[vm] * 9,
        out_specs=[vm] * 2,
        out_shape=[out, out],
        cost_estimate=pl.CostEstimate(flops=6 * vh.shape[1] * vh.shape[2] * lower.shape[1] * 2, bytes_accessed=0, transcendentals=0),
        name="second",
    )(vh, vl, wh, wl, shared, sent, lower, above, beneath)


def gathered(piece):
    count = lax.axis_size("vecs")
    groups = count // 2
    zs = [piece]
    for k in range(1, groups):
        pairs = [(d, ((d // 2 + k) % groups) * 2 + d % 2) for d in range(count)]
        zs.append(lax.ppermute(piece, "vecs", pairs))
    xs = lax.ppermute(jnp.stack(zs), "vecs", [(d, d ^ 1) for d in range(count)])
    return zs, xs


def local(vectors, reflectors):
    width = reflectors.shape[3]
    assert reflectors.shape[1] == 2 and vectors.shape[0] == 2 * width
    sections = lax.axis_size("rows")
    topmost = lax.axis_index("rows") == 0
    place = lax.axis_index("vecs").astype(jnp.int32)[None]
    up = [(r, (r - 1) % sections) for r in range(sections)]
    down = [(r, (r + 1) % sections) for r in range(sections)]
    upper, lower = vectors[:width], vectors[width:]
    tail = jnp.zeros_like(upper)
    pieces = [gathered(reflectors[t]) for t in range(reflectors.shape[0])]
    made = [prepare(place, *p) for p in pieces]
    for t in range(len(made)):
        shared = lax.ppermute(made[t][4], "rows", down)
        upper, lower = first(made[t], upper, lower)
        sent = jnp.where(topmost, tail, upper)
        beneath = lax.ppermute(sent, "rows", up)
        above = lax.ppermute(lower, "rows", down)
        updated, lower = second(made[t], shared, sent, lower, above, beneath)
        tail = updated
        upper = jnp.where(topmost, upper, updated)
    return jnp.concatenate([upper, lower], axis=0)


def solution(mesh):
    placed = (P("rows", "vecs"), P(None, "rows", "vecs", None))
    return jax.shard_map(
        local, mesh=mesh, in_specs=placed, out_specs=P("rows", "vecs"), check_vma=False
    )
```

time: 350 us -> 152 us (0.43)
  waiting for transfers between devices: 127 us -> 23.2 us
  local copies, waits for them, and re-layouts: 96.6 us -> 8.75 us
  matrix products: 74 us -> 0 us
  Pallas kernels: 0 us -> 66.4 us
  starting transfers between devices: 18.1 us -> 40.9 us
  between operations: 15.1 us -> 0.52 us
  other arithmetic: 15.6 us -> 11.2 us
    all_gather x4 -> x0, waiting for transfers between devices: 94.1 us -> none  [local(): blocks = lax.all_gather(reflectors[moment], 'vecs', axis=1, tiled=True)]
    dot_general x84 -> x0, matrix products: 74 us -> none  [the longest x28 26.2 us: invert_upper(): jnp.einsum('bij,bjk->bik', corner, right_inverse, precision=lax.Precision...]
    pallas_call x0 -> x12, Pallas kernels: none -> 66.4 us  [the longest x4 36.8 us: prepare(): pl.pallas_call(functools.partial(prepare_kernel, groups=groups), in_specs...]
    dot_general x4 -> x0, local copies, waits for them, and re-layouts: 66 us -> none  [local(): jnp.einsum('bri,brj->bij', blocks, blocks, precision=lax.Precision.HIGHEST)]
    ppermute x8 -> x28, starting transfers between devices: 18 us -> 40.9 us  [the longest x12 27.3 us: gathered(): zs.append(lax.ppermute(piece, 'vecs', pairs))]
    concatenate x58 -> x1, other arithmetic: 11.9 us -> 0.83 us  [local(): return jnp.concatenate([upper, lower], axis=0)]
    select_n x8, other arithmetic: 0.27 us -> 10.2 us  [the longest x4 6.09 us: local(): upper = jnp.where(topmost, upper, updated)]
    slice x55 -> x2, local copies, waits for them, and re-layouts: 11.8 us -> 2 us  [the longest x1 1.18 us: local(): pieces = [gathered(reflectors[t]) for t in range(reflectors.shape[0])]]
  transfers between devices with their start and end apart: 12 -> 28, of which waited for: 12 -> 6; matrix products, arithmetic and copies ran while one was open for 22% -> 7% of each run, Pallas kernels for 0% -> 41%
where the time goes in v1:
time: 152 us; the launch traced here: 151 us
  Pallas kernels  66.4 us (44%)
  starting transfers between devices  40.9 us (27%)
  waiting for transfers between devices  23.2 us (15%)
  other arithmetic  11.2 us (7%)
  local copies, waits for them, and re-layouts  8.75 us (6%)
    pallas_call x4, Pallas kernels, prepare(): pl.pallas_call(functools.partial(prepare_kernel, groups=groups), in_specs...  36.8 us
    ppermute x12, starting transfers between devices, gathered(): zs.append(lax.ppermute(piece, 'vecs', pairs))  27.3 us
    ppermute x12, waiting for transfers between devices, gathered(): zs.append(lax.ppermute(piece, 'vecs', pairs))  16.1 us
    pallas_call x4, Pallas kernels, second(): pl.pallas_call(second_kernel, in_specs=[vm] * 9, out_specs=[vm] * 2, out_...  15.6 us
    pallas_call x4, Pallas kernels, first(): pl.pallas_call(first_kernel, in_specs=[vm] * 6, out_specs=[vm] * 2, out_s...  14.1 us
    ppermute x4, waiting for transfers between devices, local(): beneath = lax.ppermute(sent, 'rows', up)  7.09 us
    ppermute x4, starting transfers between devices, local(): above = lax.ppermute(lower, 'rows', down)  6.89 us
    unnamed x90, local copies, waits for them, and re-layouts  6.75 us
  transfers between devices with their start and end apart: 28, of which 6 were waited for; matrix products, arithmetic and copies ran while one was open for 7% of the time, Pallas kernels for 41%

profile of v1, /device:TPU:1, one launch (start us, length us, event | category | flops | bytes accessed | tf_op | source)
XLA Modules:
  0.0 150.9 jit_solution(1972170209489231614)
XLA Ops:
  1.2 2.2 %collective-permute-start.12 = (f32[2,64,256]{2,1,0:T(8,128)S(1)}, f32[2,64,256]{2,1,0:T(8,128)S(1)}, u32[]{:S(2)}, u32[]{:S(2)}) collective-permute-start(f32[2,64,256]{2,1,0:T(8,128)S(1)} %get-tuple-element.83.refs_0_), channel_id=1, source_target_pairs={{0,2},{1,3},{2,4},{3,5},{4,6},{5,7},{6,0},{7,1},{8,10},{9,11},{10,... | collective-permute-start | bytes 393224 | tf_op jit(solution)/shard_map/ppermute | solution.py:167
  3.4 2.3 %collective-permute-start.13 = (f32[2,64,256]{2,1,0:T(8,128)S(1)}, f32[2,64,256]{2,1,0:T(8,128)S(1)}, u32[]{:S(2)}, u32[]{:S(2)}) collective-permute-start(f32[2,64,256]{2,1,0:T(8,128)S(1)} %get-tuple-element.83.refs_0_), channel_id=1, source_target_pairs={{0,4},{1,5},{2,6},{3,7},{4,0},{5,1},{6,2},{7,3},{8,12},{9,13},{10,... | collective-permute-start | bytes 393224 | tf_op jit(solution)/shard_map/ppermute | solution.py:167
  10.1 5.7 %collective-permute-done.13.refs_2_ = f32[2,64,256]{2,1,0:T(8,128)S(1)} collective-permute-done((f32[2,64,256]{2,1,0:T(8,128)S(1)}, f32[2,64,256]{2,1,0:T(8,128)S(1)}, u32[]{:S(2)}, u32[]{:S(2)}) %collective-permute-start.13) | collective-permute-done | bytes 131104 | tf_op jit(solution)/shard_map/ppermute | solution.py:167
  15.8 7.1 %collective-permute-start.5 = (f32[2,64,256]{2,1,0:T(8,128)S(1)}, f32[2,64,256]{2,1,0:T(8,128)S(1)}, u32[]{:S(2)}, u32[]{:S(2)}) collective-permute-start(f32[2,64,256]{2,1,0:T(8,128)S(1)} %get-tuple-element.81.refs_0_), channel_id=1, source_target_pairs={{0,4},{1,5},{2,6},{3,7},{4,0},{5,1},{6,2},{7,3},{8,12},{9,13},{10,... | collective-permute-start | bytes 393224 | tf_op jit(solution)/shard_map/ppermute | solution.py:167
  23.1 3.6 %collective-permute-start.6 = (f32[2,64,256]{2,1,0:T(8,128)S(1)}, f32[2,64,256]{2,1,0:T(8,128)S(1)}, u32[]{:S(2)}, u32[]{:S(2)}) collective-permute-start(f32[2,64,256]{2,1,0:T(8,128)S(1)} %get-tuple-element.81.refs_0_), channel_id=1, source_target_pairs={{0,6},{1,7},{2,0},{3,1},{4,2},{5,3},{6,4},{7,5},{8,14},{9,15},{10,... | collective-permute-start | bytes 393224 | tf_op jit(solution)/shard_map/ppermute | solution.py:167
  29.7 5.7 %collective-permute-start = (f32[2,64,256]{2,1,0:T(8,128)S(1)}, f32[2,64,256]{2,1,0:T(8,128)S(1)}, u32[]{:S(2)}, u32[]{:S(2)}) collective-permute-start(f32[2,64,256]{2,1,0:T(8,128)S(1)} %get-tuple-element.80.refs_0_), channel_id=1, source_target_pairs={{0,2},{1,3},{2,4},{3,5},{4,6},{5,7},{6,0},{7,1},{8,10},{9,11},{10,... | collective-permute-start | bytes 393224 | tf_op jit(solution)/shard_map/ppermute | solution.py:167
  37.1 1.9 %collective-permute-done.5.refs_2_ = f32[2,64,256]{2,1,0:T(8,128)S(1)} collective-permute-done((f32[2,64,256]{2,1,0:T(8,128)S(1)}, f32[2,64,256]{2,1,0:T(8,128)S(1)}, u32[]{:S(2)}, u32[]{:S(2)}) %collective-permute-start.5) | collective-permute-done | bytes 131104 | tf_op jit(solution)/shard_map/ppermute | solution.py:167
  38.9 1.7 %collective-permute-start.2 = (f32[2,64,256]{2,1,0:T(8,128)S(1)}, f32[2,64,256]{2,1,0:T(8,128)S(1)}, u32[]{:S(2)}, u32[]{:S(2)}) collective-permute-start(f32[2,64,256]{2,1,0:T(8,128)S(1)} %get-tuple-element.80.refs_0_), channel_id=1, source_target_pairs={{0,6},{1,7},{2,0},{3,1},{4,2},{5,3},{6,4},{7,5},{8,14},{9,15},{10,... | collective-permute-start | bytes 393224 | tf_op jit(solution)/shard_map/ppermute | solution.py:167
  42.6 6.1 %collective-permute-done.1.refs_2_ = f32[2,64,256]{2,1,0:T(8,128)S(1)} collective-permute-done((f32[2,64,256]{2,1,0:T(8,128)S(1)}, f32[2,64,256]{2,1,0:T(8,128)S(1)}, u32[]{:S(2)}, u32[]{:S(2)}) %collective-permute-start.1) | collective-permute-done | bytes 131104 | tf_op jit(solution)/shard_map/ppermute | solution.py:167
  50.7 9.2 %prepare.7 = (bf16[2,512,256]{2,1,0:T(8,128)(2,1)}, bf16[2,512,256]{2,1,0:T(8,128)(2,1)}, bf16[2,256,512]{2,1,0:T(8,128)(2,1)}, bf16[2,256,512]{2,1,0:T(8,128)(2,1)}, f32[256,512]{1,0:T(8,128)}) custom-call(s32[1]{0:T(128)} %bitcast.place_ref, f32[2,64,256]{2,1,0:T(8,128)} %copy-done.32, f32[2,64,256]{2,1,0:T(8,128)} %copy-done.42, ...), custom_call_target="tpu_custom_call" | custom-call | flops 2818572288 | bytes 2097152 | tf_op jit(solution)/shard_map/prepare/pallas_call | solution.py:96
  59.9 2.0 %collective-permute-start.16 = (f32[256,512]{1,0:T(8,128)}, f32[256,512]{1,0:T(8,128)S(1)}, u32[]{:S(2)}, u32[]{:S(2)}) collective-permute-start(f32[256,512]{1,0:T(8,128)} %get-tuple-element.58), channel_id=1, source_target_pairs={{0,8},{8,16},{16,24},{24,0},{1,9},{9,17},{17,25},{25,1},{2,10},{10... | collective-permute-start | bytes 1572872 | tf_op jit(solution)/shard_map/ppermute | solution.py:185
  61.9 3.5 %first.4 = (f32[256,256]{1,0:T(8,128)}, f32[256,256]{1,0:T(8,128)}) custom-call(bf16[2,512,256]{2,1,0:T(8,128)(2,1)} %get-tuple-element.53.vh, bf16[2,512,256]{2,1,0:T(8,128)(2,1)} %get-tuple-element.54.vl, bf16[2,256,512]{2,1,0:T(8,128)(2,1)} %get-tuple-element.55.wh, bf16[2,256,512]{2,1,0:T(8,128)(2,1)} %get-tuple-element.56.wl, ...), custom_call_target="tpu_custom_call" | custom-call | flops 402653184 | tf_op jit(solution)/shard_map/first/pallas_call | solution.py:126
  68.2 9.2 %prepare.6 = (bf16[2,512,256]{2,1,0:T(8,128)(2,1)}, bf16[2,512,256]{2,1,0:T(8,128)(2,1)}, bf16[2,256,512]{2,1,0:T(8,128)(2,1)}, bf16[2,256,512]{2,1,0:T(8,128)(2,1)}, f32[256,512]{1,0:T(8,128)}) custom-call(s32[1]{0:T(128)} %bitcast.place_ref, f32[2,64,256]{2,1,0:T(8,128)} %copy-done.31, f32[2,64,256]{2,1,0:T(8,128)} %copy-done.39, ...), custom_call_target="tpu_custom_call" | custom-call | flops 2818572288 | bytes 2097152 | tf_op jit(solution)/shard_map/prepare/pallas_call | solution.py:96
  79.0 3.9 %second.4 = (f32[256,256]{1,0:T(8,128)}, f32[256,256]{1,0:T(8,128)}) custom-call(bf16[2,512,256]{2,1,0:T(8,128)(2,1)} %get-tuple-element.53.vh, bf16[2,512,256]{2,1,0:T(8,128)(2,1)} %get-tuple-element.54.vl, bf16[2,256,512]{2,1,0:T(8,128)(2,1)} %get-tuple-element.55.wh, bf16[2,256,512]{2,1,0:T(8,128)(2,1)} %get-tuple-element.56.wl, f32[256,512]{1,0:T(8,128)} %copy-done.14, ...), custom_call_target="tpu_custom_call" | custom-call | flops 402653184 | tf_op jit(solution)/shard_map/second/pallas_call | solution.py:151
  84.6 3.6 %first.5 = (f32[256,256]{1,0:T(8,128)}, f32[256,256]{1,0:T(8,128)}) custom-call(bf16[2,512,256]{2,1,0:T(8,128)(2,1)} %get-tuple-element.49.vh, bf16[2,512,256]{2,1,0:T(8,128)(2,1)} %get-tuple-element.50.vl, bf16[2,256,512]{2,1,0:T(8,128)(2,1)} %get-tuple-element.51.wh, bf16[2,256,512]{2,1,0:T(8,128)(2,1)} %get-tuple-element.52.wl, ...), custom_call_target="tpu_custom_call" | custom-call | flops 402653184 | tf_op jit(solution)/shard_map/first/pallas_call | solution.py:126
  89.3 1.7 %collective-permute-start.20 = (f32[256,256]{1,0:T(8,128)S(1)}, f32[256,256]{1,0:T(8,128)S(1)}, u32[]{:S(2)}, u32[]{:S(2)}) collective-permute-start(f32[256,256]{1,0:T(8,128)S(1)} %copy-done.17), channel_id=1, source_target_pairs={{0,8},{8,16},{16,24},{24,0},{1,9},{9,17},{17,25},{25,1},{2,10},{10... | collective-permute-start | bytes 786440 | tf_op jit(solution)/shard_map/ppermute | solution.py:189
  91.0 9.2 %prepare.5 = (bf16[2,512,256]{2,1,0:T(8,128)(2,1)}, bf16[2,512,256]{2,1,0:T(8,128)(2,1)}, bf16[2,256,512]{2,1,0:T(8,128)(2,1)}, bf16[2,256,512]{2,1,0:T(8,128)(2,1)}, f32[256,512]{1,0:T(8,128)}) custom-call(s32[1]{0:T(128)} %bitcast.place_ref, f32[2,64,256]{2,1,0:T(8,128)} %copy-done.30, f32[2,64,256]{2,1,0:T(8,128)} %copy-done.36, ...), custom_call_target="tpu_custom_call" | custom-call | flops 2818572288 | bytes 2097152 | tf_op jit(solution)/shard_map/prepare/pallas_call | solution.py:96
  102.0 3.9 %second.5 = (f32[256,256]{1,0:T(8,128)}, f32[256,256]{1,0:T(8,128)}) custom-call(bf16[2,512,256]{2,1,0:T(8,128)(2,1)} %get-tuple-element.49.vh, bf16[2,512,256]{2,1,0:T(8,128)(2,1)} %get-tuple-element.50.vl, bf16[2,256,512]{2,1,0:T(8,128)(2,1)} %get-tuple-element.51.wh, bf16[2,256,512]{2,1,0:T(8,128)(2,1)} %get-tuple-element.52.wl, f32[256,512]{1,0:T(8,128)} %copy-done.12, ...), custom_call_target="tpu_custom_call" | custom-call | flops 402653184 | tf_op jit(solution)/shard_map/second/pallas_call | solution.py:151
  107.6 3.5 %first.6 = (f32[256,256]{1,0:T(8,128)}, f32[256,256]{1,0:T(8,128)}) custom-call(bf16[2,512,256]{2,1,0:T(8,128)(2,1)} %get-tuple-element.45.vh, bf16[2,512,256]{2,1,0:T(8,128)(2,1)} %get-tuple-element.46.vl, bf16[2,256,512]{2,1,0:T(8,128)(2,1)} %get-tuple-element.47.wh, bf16[2,256,512]{2,1,0:T(8,128)(2,1)} %get-tuple-element.48.wl, ...), custom_call_target="tpu_custom_call" | custom-call | flops 402653184 | tf_op jit(solution)/shard_map/first/pallas_call | solution.py:126
  113.9 9.2 %prepare.4 = (bf16[2,512,256]{2,1,0:T(8,128)(2,1)}, bf16[2,512,256]{2,1,0:T(8,128)(2,1)}, bf16[2,256,512]{2,1,0:T(8,128)(2,1)}, bf16[2,256,512]{2,1,0:T(8,128)(2,1)}, f32[256,512]{1,0:T(8,128)}) custom-call(s32[1]{0:T(128)} %bitcast.place_ref, f32[2,64,256]{2,1,0:T(8,128)} %copy-done.29, f32[2,64,256]{2,1,0:T(8,128)} %copy-done.33, ...), custom_call_target="tpu_custom_call" | custom-call | flops 2818572288 | bytes 2097152 | tf_op jit(solution)/shard_map/prepare/pallas_call | solution.py:96
  124.7 3.9 %second.6 = (f32[256,256]{1,0:T(8,128)}, f32[256,256]{1,0:T(8,128)}) custom-call(bf16[2,512,256]{2,1,0:T(8,128)(2,1)} %get-tuple-element.45.vh, bf16[2,512,256]{2,1,0:T(8,128)(2,1)} %get-tuple-element.46.vl, bf16[2,256,512]{2,1,0:T(8,128)(2,1)} %get-tuple-element.47.wh, bf16[2,256,512]{2,1,0:T(8,128)(2,1)} %get-tuple-element.48.wl, f32[256,512]{1,0:T(8,128)} %copy-done.11, ...), custom_call_target="tpu_custom_call" | custom-call | flops 402653184 | tf_op jit(solution)/shard_map/second/pallas_call | solution.py:151
  130.3 3.5 %first.7 = (f32[256,256]{1,0:T(8,128)}, f32[256,256]{1,0:T(8,128)}) custom-call(bf16[2,512,256]{2,1,0:T(8,128)(2,1)} %get-tuple-element.41.vh, bf16[2,512,256]{2,1,0:T(8,128)(2,1)} %get-tuple-element.42.vl, bf16[2,256,512]{2,1,0:T(8,128)(2,1)} %get-tuple-element.43.wh, bf16[2,256,512]{2,1,0:T(8,128)(2,1)} %get-tuple-element.44.wl, ...), custom_call_target="tpu_custom_call" | custom-call | flops 402653184 | tf_op jit(solution)/shard_map/first/pallas_call | solution.py:126
  136.7 7.1 %collective-permute-done.27.beneath = f32[256,256]{1,0:T(8,128)S(1)} collective-permute-done((f32[256,256]{1,0:T(8,128)S(1)}, f32[256,256]{1,0:T(8,128)S(1)}, u32[]{:S(2)}, u32[]{:S(2)}) %collective-permute-start.27) | collective-permute-done | bytes 262176 | tf_op jit(solution)/shard_map/ppermute | solution.py:188
  145.2 3.9 %second.7 = (f32[256,256]{1,0:T(8,128)}, f32[256,256]{1,0:T(8,128)}) custom-call(bf16[2,512,256]{2,1,0:T(8,128)(2,1)} %get-tuple-element.41.vh, bf16[2,512,256]{2,1,0:T(8,128)(2,1)} %get-tuple-element.42.vl, bf16[2,256,512]{2,1,0:T(8,128)(2,1)} %get-tuple-element.43.wh, bf16[2,256,512]{2,1,0:T(8,128)(2,1)} %get-tuple-element.44.wl, f32[256,512]{1,0:T(8,128)} %copy-done.13, ...), custom_call_target="tpu_custom_call" | custom-call | flops 402653184 | tf_op jit(solution)/shard_map/second/pallas_call | solution.py:151
  (149 shorter events, 36.8 us)
Async XLA Ops:
  3.4 12.4 %collective-permute-start.13 = (f32[2,64,256]{2,1,0:T(8,128)S(1)}, f32[2,64,256]{2,1,0:T(8,128)S(1)}, u32[]{:S(2)}, u32[]{:S(2)}) collective-permute-start(f32[2,64,256]{2,1,0:T(8,128)S(1)} %get-tuple-element.83.refs_0_), channel_id=1, source_target_pairs={{0,4},{1,5},{2,6},{3,7},{4,0},{5,1},{6,2},{7,3},{8,12},{9,13},{10,... | collective-permute-start | bytes 393224 | tf_op jit(solution)/shard_map/ppermute | solution.py:167
  5.7 10.1 %collective-permute-start.14 = (f32[2,64,256]{2,1,0:T(8,128)S(1)}, f32[2,64,256]{2,1,0:T(8,128)S(1)}, u32[]{:S(2)}, u32[]{:S(2)}) collective-permute-start(f32[2,64,256]{2,1,0:T(8,128)S(1)} %get-tuple-element.83.refs_0_), channel_id=1, source_target_pairs={{0,6},{1,7},{2,0},{3,1},{4,2},{5,3},{6,4},{7,5},{8,14},{9,15},{10,... | collective-permute-start | bytes 393224 | tf_op jit(solution)/shard_map/ppermute | solution.py:167
  6.8 16.3 %collective-permute-start.8 = (f32[2,64,256]{2,1,0:T(8,128)S(1)}, f32[2,64,256]{2,1,0:T(8,128)S(1)}, u32[]{:S(2)}, u32[]{:S(2)}) collective-permute-start(f32[2,64,256]{2,1,0:T(8,128)S(1)} %get-tuple-element.82.refs_0_), channel_id=1, source_target_pairs={{0,2},{1,3},{2,4},{3,5},{4,6},{5,7},{6,0},{7,1},{8,10},{9,11},{10,... | collective-permute-start | bytes 393224 | tf_op jit(solution)/shard_map/ppermute | solution.py:167
  7.2 20.5 %collective-permute-start.9 = (f32[2,64,256]{2,1,0:T(8,128)S(1)}, f32[2,64,256]{2,1,0:T(8,128)S(1)}, u32[]{:S(2)}, u32[]{:S(2)}) collective-permute-start(f32[2,64,256]{2,1,0:T(8,128)S(1)} %get-tuple-element.82.refs_0_), channel_id=1, source_target_pairs={{0,4},{1,5},{2,6},{3,7},{4,0},{5,1},{6,2},{7,3},{8,12},{9,13},{10,... | collective-permute-start | bytes 393224 | tf_op jit(solution)/shard_map/ppermute | solution.py:167
  8.6 21.1 %collective-permute-start.10 = (f32[2,64,256]{2,1,0:T(8,128)S(1)}, f32[2,64,256]{2,1,0:T(8,128)S(1)}, u32[]{:S(2)}, u32[]{:S(2)}) collective-permute-start(f32[2,64,256]{2,1,0:T(8,128)S(1)} %get-tuple-element.82.refs_0_), channel_id=1, source_target_pairs={{0,6},{1,7},{2,0},{3,1},{4,2},{5,3},{6,4},{7,5},{8,14},{9,15},{10,... | collective-permute-start | bytes 393224 | tf_op jit(solution)/shard_map/ppermute | solution.py:167
  15.8 19.7 %collective-permute-start.4 = (f32[2,64,256]{2,1,0:T(8,128)S(1)}, f32[2,64,256]{2,1,0:T(8,128)S(1)}, u32[]{:S(2)}, u32[]{:S(2)}) collective-permute-start(f32[2,64,256]{2,1,0:T(8,128)S(1)} %get-tuple-element.81.refs_0_), channel_id=1, source_target_pairs={{0,2},{1,3},{2,4},{3,5},{4,6},{5,7},{6,0},{7,1},{8,10},{9,11},{10,... | collective-permute-start | bytes 393224 | tf_op jit(solution)/shard_map/ppermute | solution.py:167
  15.8 23.1 %collective-permute-start.5 = (f32[2,64,256]{2,1,0:T(8,128)S(1)}, f32[2,64,256]{2,1,0:T(8,128)S(1)}, u32[]{:S(2)}, u32[]{:S(2)}) collective-permute-start(f32[2,64,256]{2,1,0:T(8,128)S(1)} %get-tuple-element.81.refs_0_), channel_id=1, source_target_pairs={{0,4},{1,5},{2,6},{3,7},{4,0},{5,1},{6,2},{7,3},{8,12},{9,13},{10,... | collective-permute-start | bytes 393224 | tf_op jit(solution)/shard_map/ppermute | solution.py:167
  23.1 17.7 %collective-permute-start.6 = (f32[2,64,256]{2,1,0:T(8,128)S(1)}, f32[2,64,256]{2,1,0:T(8,128)S(1)}, u32[]{:S(2)}, u32[]{:S(2)}) collective-permute-start(f32[2,64,256]{2,1,0:T(8,128)S(1)} %get-tuple-element.81.refs_0_), channel_id=1, source_target_pairs={{0,6},{1,7},{2,0},{3,1},{4,2},{5,3},{6,4},{7,5},{8,14},{9,15},{10,... | collective-permute-start | bytes 393224 | tf_op jit(solution)/shard_map/ppermute | solution.py:167
  27.7 23.0 %collective-permute-start.15 = (f32[4,2,64,256]{3,2,1,0:T(8,128)S(1)}, f32[4,2,64,256]{3,2,1,0:T(8,128)}, u32[]{:S(2)}, u32[]{:S(2)}) collective-permute-start(f32[4,2,64,256]{3,2,1,0:T(8,128)S(1)} %pad_maximum_fusion.3), channel_id=1, source_target_pairs={{0,1},{1,0},{2,3},{3,2},{4,5},{5,4},{6,7},{7,6},{8,9},{9,8},{10,11... | collective-permute-start | bytes 1572872 | tf_op jit(solution)/shard_map/ppermute | solution.py:168
  29.7 12.4 %collective-permute-start = (f32[2,64,256]{2,1,0:T(8,128)S(1)}, f32[2,64,256]{2,1,0:T(8,128)S(1)}, u32[]{:S(2)}, u32[]{:S(2)}) collective-permute-start(f32[2,64,256]{2,1,0:T(8,128)S(1)} %get-tuple-element.80.refs_0_), channel_id=1, source_target_pairs={{0,2},{1,3},{2,4},{3,5},{4,6},{5,7},{6,0},{7,1},{8,10},{9,11},{10,... | collective-permute-start | bytes 393224 | tf_op jit(solution)/shard_map/ppermute | solution.py:167
  35.5 13.3 %collective-permute-start.1 = (f32[2,64,256]{2,1,0:T(8,128)S(1)}, f32[2,64,256]{2,1,0:T(8,128)S(1)}, u32[]{:S(2)}, u32[]{:S(2)}) collective-permute-start(f32[2,64,256]{2,1,0:T(8,128)S(1)} %get-tuple-element.80.refs_0_), channel_id=1, source_target_pairs={{0,4},{1,5},{2,6},{3,7},{4,0},{5,1},{6,2},{7,3},{8,12},{9,13},{10,... | collective-permute-start | bytes 393224 | tf_op jit(solution)/shard_map/ppermute | solution.py:167
  40.8 25.7 %collective-permute-start.11 = (f32[4,2,64,256]{3,2,1,0:T(8,128)S(1)}, f32[4,2,64,256]{3,2,1,0:T(8,128)}, u32[]{:S(2)}, u32[]{:S(2)}) collective-permute-start(f32[4,2,64,256]{3,2,1,0:T(8,128)S(1)} %pad_maximum_fusion.2), channel_id=1, source_target_pairs={{0,1},{1,0},{2,3},{3,2},{4,5},{5,4},{6,7},{7,6},{8,9},{9,8},{10,11... | collective-permute-start | bytes 1572872 | tf_op jit(solution)/shard_map/ppermute | solution.py:168
  42.1 48.9 %collective-permute-start.7 = (f32[4,2,64,256]{3,2,1,0:T(8,128)S(1)}, f32[4,2,64,256]{3,2,1,0:T(8,128)}, u32[]{:S(2)}, u32[]{:S(2)}) collective-permute-start(f32[4,2,64,256]{3,2,1,0:T(8,128)S(1)} %pad_maximum_fusion.1), channel_id=1, source_target_pairs={{0,1},{1,0},{2,3},{3,2},{4,5},{5,4},{6,7},{7,6},{8,9},{9,8},{10,11... | collective-permute-start | bytes 1572872 | tf_op jit(solution)/shard_map/ppermute | solution.py:168
  49.4 64.5 %collective-permute-start.3 = (f32[4,2,64,256]{3,2,1,0:T(8,128)S(1)}, f32[4,2,64,256]{3,2,1,0:T(8,128)}, u32[]{:S(2)}, u32[]{:S(2)}) collective-permute-start(f32[4,2,64,256]{3,2,1,0:T(8,128)S(1)} %pad_maximum_fusion), channel_id=1, source_target_pairs={{0,1},{1,0},{2,3},{3,2},{4,5},{5,4},{6,7},{7,6},{8,9},{9,8},{10,11... | collective-permute-start | bytes 1572872 | tf_op jit(solution)/shard_map/ppermute | solution.py:168
  59.9 17.6 %collective-permute-start.16 = (f32[256,512]{1,0:T(8,128)}, f32[256,512]{1,0:T(8,128)S(1)}, u32[]{:S(2)}, u32[]{:S(2)}) collective-permute-start(f32[256,512]{1,0:T(8,128)} %get-tuple-element.58), channel_id=1, source_target_pairs={{0,8},{8,16},{16,24},{24,0},{1,9},{9,17},{17,25},{25,1},{2,10},{10... | collective-permute-start | bytes 1572872 | tf_op jit(solution)/shard_map/ppermute | solution.py:185
  66.4 11.0 %collective-permute-start.18 = (f32[256,256]{1,0:T(8,128)S(1)}, f32[256,256]{1,0:T(8,128)S(1)}, u32[]{:S(2)}, u32[]{:S(2)}) collective-permute-start(f32[256,256]{1,0:T(8,128)S(1)} %broadcast_select_fusion.sent), channel_id=1, source_target_pairs={{0,24},{8,0},{16,8},{24,16},{1,25},{9,1},{17,9},{25,17},{2,26},{10... | collective-permute-start | bytes 786440 | tf_op jit(solution)/shard_map/ppermute | solution.py:188
  66.5 11.0 %collective-permute-start.17 = (f32[256,256]{1,0:T(8,128)S(1)}, f32[256,256]{1,0:T(8,128)S(1)}, u32[]{:S(2)}, u32[]{:S(2)}) collective-permute-start(f32[256,256]{1,0:T(8,128)S(1)} %copy-done.18), channel_id=1, source_target_pairs={{0,8},{8,16},{16,24},{24,0},{1,9},{9,17},{17,25},{25,1},{2,10},{10... | collective-permute-start | bytes 786440 | tf_op jit(solution)/shard_map/ppermute | solution.py:189
  77.4 23.0 %collective-permute-start.19 = (f32[256,512]{1,0:T(8,128)}, f32[256,512]{1,0:T(8,128)S(1)}, u32[]{:S(2)}, u32[]{:S(2)}) collective-permute-start(f32[256,512]{1,0:T(8,128)} %get-tuple-element.63), channel_id=1, source_target_pairs={{0,8},{8,16},{16,24},{24,0},{1,9},{9,17},{17,25},{25,1},{2,10},{10... | collective-permute-start | bytes 1572872 | tf_op jit(solution)/shard_map/ppermute | solution.py:185
  89.2 11.2 %collective-permute-start.21 = (f32[256,256]{1,0:T(8,128)S(1)}, f32[256,256]{1,0:T(8,128)S(1)}, u32[]{:S(2)}, u32[]{:S(2)}) collective-permute-start(f32[256,256]{1,0:T(8,128)S(1)} %broadcast_select_fusion.6.sent), channel_id=1, source_target_pairs={{0,24},{8,0},{16,8},{24,16},{1,25},{9,1},{17,9},{25,17},{2,26},{10... | collective-permute-start | bytes 786440 | tf_op jit(solution)/shard_map/ppermute | solution.py:188
  89.3 11.2 %collective-permute-start.20 = (f32[256,256]{1,0:T(8,128)S(1)}, f32[256,256]{1,0:T(8,128)S(1)}, u32[]{:S(2)}, u32[]{:S(2)}) collective-permute-start(f32[256,256]{1,0:T(8,128)S(1)} %copy-done.17), channel_id=1, source_target_pairs={{0,8},{8,16},{16,24},{24,0},{1,9},{9,17},{17,25},{25,1},{2,10},{10... | collective-permute-start | bytes 786440 | tf_op jit(solution)/shard_map/ppermute | solution.py:189
  100.2 22.9 %collective-permute-start.22 = (f32[256,512]{1,0:T(8,128)}, f32[256,512]{1,0:T(8,128)S(1)}, u32[]{:S(2)}, u32[]{:S(2)}) collective-permute-start(f32[256,512]{1,0:T(8,128)} %get-tuple-element.68), channel_id=1, source_target_pairs={{0,8},{8,16},{16,24},{24,0},{1,9},{9,17},{17,25},{25,1},{2,10},{10... | collective-permute-start | bytes 1572872 | tf_op jit(solution)/shard_map/ppermute | solution.py:185
  112.1 11.0 %collective-permute-start.24 = (f32[256,256]{1,0:T(8,128)S(1)}, f32[256,256]{1,0:T(8,128)S(1)}, u32[]{:S(2)}, u32[]{:S(2)}) collective-permute-start(f32[256,256]{1,0:T(8,128)S(1)} %broadcast_select_fusion.4.sent), channel_id=1, source_target_pairs={{0,24},{8,0},{16,8},{24,16},{1,25},{9,1},{17,9},{25,17},{2,26},{10... | collective-permute-start | bytes 786440 | tf_op jit(solution)/shard_map/ppermute | solution.py:188
  112.2 11.0 %collective-permute-start.23 = (f32[256,256]{1,0:T(8,128)S(1)}, f32[256,256]{1,0:T(8,128)S(1)}, u32[]{:S(2)}, u32[]{:S(2)}) collective-permute-start(f32[256,256]{1,0:T(8,128)S(1)} %copy-done.16), channel_id=1, source_target_pairs={{0,8},{8,16},{16,24},{24,0},{1,9},{9,17},{17,25},{25,1},{2,10},{10... | collective-permute-start | bytes 786440 | tf_op jit(solution)/shard_map/ppermute | solution.py:189
  123.1 13.6 %collective-permute-start.25 = (f32[256,512]{1,0:T(8,128)}, f32[256,512]{1,0:T(8,128)S(1)}, u32[]{:S(2)}, u32[]{:S(2)}) collective-permute-start(f32[256,512]{1,0:T(8,128)} %get-tuple-element.73), channel_id=1, source_target_pairs={{0,8},{8,16},{16,24},{24,0},{1,9},{9,17},{17,25},{25,1},{2,10},{10... | collective-permute-start | bytes 1572872 | tf_op jit(solution)/shard_map/ppermute | solution.py:185
  (49 other events, 337.8 us)
